TPU v7x, 32 devices: a whole 2x2x4 slice. The times are simulated.
32 devices in a mesh: groups: 2 (over y), res: 8 (over z, x), seq: 2 (over core).
Axes of the slice: x: 2, y: 2, z: 4, core: 2. Of those that a mesh axis runs over, the one named last changes fastest.
Arguments:
- alignment: bfloat16 [128, 32, 256], P(('groups', 'seq'), 'res'), parts along dimension 0, may hold values from -6 to 6
- ln_gain: float32 [256], replicated, may hold values from 0.1 to 1.9
- proj_left: bfloat16 [256, 32], replicated, may hold values from -0.375 to 0.375
- proj_right: bfloat16 [256, 32], replicated, may hold values from -0.375 to 0.375
- out_weight: bfloat16 [1024, 128], replicated, may hold values from -4 to 4
- out_bias: float32 [128], replicated, may hold values from -3 to 3
Outputs:
- pair_update: bfloat16 [64, 32, 128], P(('groups', 'res'), 'seq'), parts along dimension 0
There are 2 independent parts, one for each index of `groups`. A program takes and returns all parts, laid end to end along the dimension named above; an argument that names none is the same for every part. Nothing has to cross between parts.
All inputs are finite; a program needn't handle non-finite values.
Results may differ from a plain program's by a relative error of at most 0.0095.
Values may be sent and summed in bfloat16 or wider, within the bound.
No kernel may reach another device: no remote copies, remote signals or barrier semaphores. Data moves between devices by JAX's collectives and lax.ppermute only.
A program may use at most 64 MiB of HBM per device.

v0:
```python
import math
import jax
import jax.numpy as jnp
from jax import lax
from jax.sharding import PartitionSpec as P


def normalize(alignment, ln_gain):
    values = alignment.astype(jnp.float32)
    centred = values - jnp.mean(values, axis=-1, keepdims=True)
    variance = jnp.mean(centred * centred, axis=-1, keepdims=True)
    return (centred * lax.rsqrt(variance + 1e-05) * ln_gain).astype(jnp.bfloat16)


def pair_block(left_flat, columns, weight_full, inv_count):
    channels = columns.shape[2]
    col_count = columns.shape[1]
    row_count = left_flat.shape[1] // channels
    block_width = math.gcd(col_count, 64)

    def advance(position, totals):
        column_block = lax.dynamic_slice_in_dim(columns, position * block_width, block_width, 1)
        right_flat = column_block.reshape(columns.shape[0], block_width * channels)
        outer_terms = (
            lax.dot_general(
                left_flat, right_flat, (((0,), (0,)), ((), ())), preferred_element_type=jnp.float32
            )
            * inv_count
        )
        outer_terms = outer_terms.reshape(row_count, channels, block_width, channels).transpose(
            0, 2, 1, 3
        )
        outer_terms = outer_terms.reshape(row_count * block_width, channels * channels)
        projected = jnp.dot(outer_terms, weight_full, precision=lax.Precision.HIGHEST)
        projected = projected.reshape(row_count, block_width, weight_full.shape[1])
        return lax.dynamic_update_slice_in_dim(totals, projected, position * block_width, 1)

    totals = jnp.zeros((row_count, col_count, weight_full.shape[1]), jnp.float32)
    return lax.fori_loop(0, col_count // block_width, advance, totals)


def on_device(alignment, ln_gain, proj_left, proj_right, out_weight, out_bias):
    seq_shards = lax.axis_size("seq")
    local_seqs = alignment.shape[0]
    local_res = alignment.shape[1]
    channels = proj_left.shape[1]
    inv_count = 1.0 / (local_seqs * seq_shards)
    normed = normalize(alignment, ln_gain)
    flat_rows = normed.reshape(-1, normed.shape[2])
    both_sides = jnp.dot(
        flat_rows, jnp.concatenate((proj_left, proj_right), 1), preferred_element_type=jnp.float32
    )
    both_sides = both_sides.astype(jnp.bfloat16).reshape(local_seqs, local_res, 2 * channels)
    left_side = both_sides[:, :, :channels]
    right_side = both_sides[:, :, channels:]
    weight_full = out_weight.astype(jnp.float32)
    left_all = lax.all_gather(left_side, "seq", axis=0, tiled=True)
    left_flat = left_all.reshape(left_all.shape[0], local_res * channels)
    right_all = lax.all_gather(right_side, "res", axis=1, tiled=True)
    split_right = right_all.reshape(
        local_seqs, seq_shards, right_all.shape[1] // seq_shards, channels
    )
    arrived = lax.all_to_all(split_right, "seq", split_axis=1, concat_axis=0, tiled=True)
    squeezed = arrived.reshape(arrived.shape[0], arrived.shape[2], arrived.shape[3])
    summed = pair_block(left_flat, squeezed, weight_full, inv_count)
    return (summed + out_bias).astype(jnp.bfloat16)


def solution(mesh):
    placed = (P(("groups", "seq"), "res", None), P(), P(), P(), P(), P())
    return jax.shard_map(
        on_device,
        mesh=mesh,
        in_specs=placed,
        out_specs=P(("groups", "res"), "seq", None),
        check_vma=False,
    )
```

profile of v0, /device:TPU:0, one launch (start us, length us, event | category | flops | bytes accessed | tf_op | source)
XLA Modules:
  0.0 44.9 jit_solution(8482532180802499849)
XLA Ops:
  0.0 0.0 copy-start
  0.0 0.0 copy-start.1
  0.0 1.0 %convert_reduce_fusion = f32[32,4]{1,0:T(8,128)S(1)} fusion(bf16[32,4,256]{2,1,0:T(4,128)(2,1)} %param.6), kind=kLoop, calls=%fused_computation.6 | loop fusion | flops 65408 | bytes 66048 | tf_op jit(solution)/shard_map/reduce_sum | solution.py:10
  1.0 0.0 copy-done.1
  1.1 0.2 fusion.4
  1.2 0.0 copy-start.4
  1.3 0.7 %copy-done.4 = f32[256]{0:T(256)S(1)} copy-done((f32[256]{0:T(256)S(1)}, f32[256]{0:T(256)}, u32[]{:S(2)}) %copy-start.4) | copy-done | bytes 1048
  1.9 0.1 fusion.6
  2.1 0.0 copy-start.2
  2.1 0.0 copy-start.3
  2.1 0.7 %copy-done.2 = bf16[256,32]{0,1:T(8,128)(2,1)S(1)} copy-done((bf16[256,32]{0,1:T(8,128)(2,1)S(1)}, bf16[256,32]{0,1:T(8,128)(2,1)}, u32[]{:S(2)}) %copy-start.2) | copy-done | bytes 16408
  2.8 0.0 copy-done.3
  2.8 0.1 convolution_convert_fusion
  2.9 0.1 copy.12
  3.1 0.1 fusion.11
  3.2 32.6 %all_gather.7 = bf16[32,32,32]{2,0,1:T(8,128)(2,1)S(1)} all-gather(bf16[32,4,32]{2,0,1:T(8,128)(2,1)S(1)} %copy.14), channel_id=1, replica_groups=mesh['groups'=2,'res'=8,'seq'=2] {'res'}, dimensions={1}, use_global_device_ids=true | all-gather | bytes 73728 | tf_op jit(solution)/shard_map/all_gather | solution.py:59
  35.7 0.1 copy.21
  35.9 0.9 %reshape.50 = bf16[2,2,8192]{2,1,0:T(2,128)(2,1)} reshape(bf16[2,32,16,32]{3,2,1,0:T(8,128)(2,1)S(1)} %bitcast.27) | data formatting | bytes 131072
  36.8 3.3 %all-to-all-start = ((bf16[2,2,8192]{2,1,0:T(2,128)(2,1)}), bf16[2,2,8192]{2,1,0:T(2,128)(2,1)S(1)}, u32[]{:S(2)}, u32[]{:S(2)}) async-start(bf16[2,2,8192]{2,1,0:T(2,128)(2,1)} %reshape.50), calls=%async_computation | async-start | bytes 131072 | tf_op jit(solution)/shard_map/all_to_all | solution.py:63
  40.1 2.0 %all_gather.6 = bf16[64,4,32]{2,1,0:T(4,128)(2,1)S(1)} all-gather(bf16[32,4,32]{2,1,0:T(4,128)(2,1)S(1)} %get-tuple-element.16), channel_id=1, replica_groups=mesh['groups'=2,'res'=8,'seq'=2] {'seq'}, dimensions={0}, use_global_device_ids=true | all-gather | bytes 24576 | tf_op jit(solution)/shard_map/all_gather | solution.py:57
  42.0 0.1 copy.13
  42.1 0.0 all-to-all-done
  42.2 0.2 reshape.51
  42.4 0.2 reshape.47
  42.6 0.2 convolution_multiply_fusion
  42.8 0.3 reshape.48
  43.1 0.3 copy.17
  43.4 0.0 copy-start.5
  43.4 0.5 %dot_general.15 = f32[4,16,1024]{2,1,0:T(8,128)S(1)} reshape(f32[4,16,32,32]{3,2,1,0:T(8,128)S(1)} %copy.17) | data formatting | bytes 524288 | tf_op jit(solution)/shard_map/while/body/eval_jaxpr/dot_general | solution.py:34
  43.9 0.0 copy-done
  43.9 0.1 copy-done.5
  44.0 0.9 %fusion = bf16[4,16,128]{2,1,0:T(8,128)(2,1)} fusion(f32[4,16,1024]{2,1,0:T(8,128)S(1)} %dot_general.15, bf16[1024,128]{1,0:T(8,128)(2,1)S(1)} %copy-done, f32[128]{0:T(128)S(1)} %copy-done.5), kind=kOutput, calls=%fused_computation.3 | convolution fusion | flops 100679680 | bytes 541184 | tf_op jit(solution)/shard_map/while/body/eval_jaxpr/dot_general | solution.py:34
  (5 shorter events, 0.1 us)
Async XLA Ops:
  0.0 43.9 %copy-start = (bf16[1024,128]{1,0:T(8,128)(2,1)S(1)}, bf16[1024,128]{1,0:T(8,128)(2,1)}, u32[]{:S(2)}) copy-start(bf16[1024,128]{1,0:T(8,128)(2,1)} %param.10) | copy-start | bytes 786436
  0.0 1.0 %copy-start.1 = (bf16[32,4,256]{2,1,0:T(4,128)(2,1)S(1)}, bf16[32,4,256]{2,1,0:T(4,128)(2,1)}, u32[]{:S(2)}) copy-start(bf16[32,4,256]{2,1,0:T(4,128)(2,1)} %param.6) | copy-start | bytes 196612
  1.2 0.7 %copy-start.4 = (f32[256]{0:T(256)S(1)}, f32[256]{0:T(256)}, u32[]{:S(2)}) copy-start(f32[256]{0:T(256)} %param.7) | copy-start | bytes 3076
  2.1 0.7 %copy-start.2 = (bf16[256,32]{0,1:T(8,128)(2,1)S(1)}, bf16[256,32]{0,1:T(8,128)(2,1)}, u32[]{:S(2)}) copy-start(bf16[256,32]{0,1:T(8,128)(2,1)} %param.9) | copy-start | bytes 49156
  2.1 0.7 %copy-start.3 = (bf16[256,32]{0,1:T(8,128)(2,1)S(1)}, bf16[256,32]{0,1:T(8,128)(2,1)}, u32[]{:S(2)}) copy-start(bf16[256,32]{0,1:T(8,128)(2,1)} %param.8) | copy-start | bytes 49156
  36.8 5.4 %all-to-all-start = ((bf16[2,2,8192]{2,1,0:T(2,128)(2,1)}), bf16[2,2,8192]{2,1,0:T(2,128)(2,1)S(1)}, u32[]{:S(2)}, u32[]{:S(2)}) async-start(bf16[2,2,8192]{2,1,0:T(2,128)(2,1)} %reshape.50), calls=%async_computation | async-start | bytes 131072 | tf_op jit(solution)/shard_map/all_to_all | solution.py:63
  43.4 0.7 %copy-start.5 = (f32[128]{0:T(128)S(1)}, f32[128]{0:T(128)}, u32[]{:S(2)}) copy-start(f32[128]{0:T(128)} %param.11) | copy-start | bytes 1540
where the time goes:
time: 45.3 us; the launch traced here: 44.9 us
  blocking collectives  34.5 us (76%)
  local copies, waits for them, and re-layouts  4.41 us (10%)
  starting transfers between devices  3.29 us (7%)
  other arithmetic  1.34 us (3%)
  matrix products  1.15 us (3%)
    all_gather x1, blocking collectives, on_device(): right_all = lax.all_gather(right_side, 'res', axis=1, tiled=True)  32.6 us
    all_to_all x1, starting transfers between devices, on_device(): lax.all_to_all(split_right, 'seq', split_axis=1, concat_axis=0, tiled=True)  3.29 us
    unnamed x14, local copies, waits for them, and re-layouts  2.61 us
    all_gather x1, blocking collectives, on_device(): left_all = lax.all_gather(left_side, 'seq', axis=0, tiled=True)  1.98 us
    reduce_sum x1, other arithmetic, normalize(): centred = values - jnp.mean(values, axis=-1, keepdims=True)  1.02 us
  transfers between devices with their start and end apart: 1, of which 0 were waited for; matrix products, arithmetic and copies ran while one was open for 0% of the time, Pallas kernels for 0%

commit v1 on v0

--- a/solution.py
+++ b/solution.py
@@ -56,7 +56,13 @@
     weight_full = out_weight.astype(jnp.float32)
     left_all = lax.all_gather(left_side, "seq", axis=0, tiled=True)
     left_flat = left_all.reshape(left_all.shape[0], local_res * channels)
-    right_all = lax.all_gather(right_side, "res", axis=1, tiled=True)
+    n_dev = lax.axis_size("res")
+    held, blocks = (right_side, [right_side])
+    for _ in range(n_dev - 1):
+        held = lax.ppermute(held, "res", [(i, (i + 1) % n_dev) for i in range(n_dev)])
+        blocks.insert(0, held)
+    line = jnp.concatenate(blocks, axis=1)
+    right_all = jnp.roll(line, (lax.axis_index("res") + 1) * right_side.shape[1], axis=1)
     split_right = right_all.reshape(
         local_seqs, seq_shards, right_all.shape[1] // seq_shards, channels
     )

time: 45.3 us -> 59.1 us (1.30)
  waiting for transfers between devices: 0.01 us -> 43 us
  blocking collectives: 34.5 us -> 5.63 us
    ppermute x0 -> x7, waiting for transfers between devices: none -> 43 us  [on_device(): lax.ppermute(held, 'res', [(i, (i + 1) % n_dev) for i in range(n_dev)])]
    all_gather x1 -> x0, blocking collectives: 32.6 us -> none  [on_device(): right_all = lax.all_gather(right_side, 'res', axis=1, tiled=True)]
    all_to_all x0 -> x1, blocking collectives: none -> 3.79 us  [on_device(): lax.all_to_all(split_right, 'seq', split_axis=1, concat_axis=0, tiled=True)]
    all_to_all x1 -> x0, starting transfers between devices: 3.29 us -> none  [on_device(): lax.all_to_all(split_right, 'seq', split_axis=1, concat_axis=0, tiled=True)]
    ppermute x0 -> x7, starting transfers between devices: none -> 3.04 us  [on_device(): lax.ppermute(held, 'res', [(i, (i + 1) % n_dev) for i in range(n_dev)])]
    unnamed x14, local copies, waits for them, and re-layouts: 2.61 us -> 1.99 us
  transfers between devices with their start and end apart: 1 -> 7, of which waited for: 0 -> 7; matrix products, arithmetic and copies ran while one was open for 0% -> 0% of each run, Pallas kernels for 0% -> 0%
where the time goes in v1:
time: 59.1 us; the launch traced here: 58.7 us
  waiting for transfers between devices  43 us (73%)
  blocking collectives  5.63 us (10%)
  local copies, waits for them, and re-layouts  4.36 us (7%)
  starting transfers between devices  3.04 us (5%)
  other arithmetic  1.34 us (2%)
  matrix products  1.16 us (2%)
    ppermute x7, waiting for transfers between devices, on_device(): lax.ppermute(held, 'res', [(i, (i + 1) % n_dev) for i in range(n_dev)])  43 us
    all_to_all x1, blocking collectives, on_device(): lax.all_to_all(split_right, 'seq', split_axis=1, concat_axis=0, tiled=True)  3.79 us
    ppermute x7, starting transfers between devices, on_device(): lax.ppermute(held, 'res', [(i, (i + 1) % n_dev) for i in range(n_dev)])  3.04 us
    unnamed x14, local copies, waits for them, and re-layouts  1.99 us
    all_gather x1, blocking collectives, on_device(): left_all = lax.all_gather(left_side, 'seq', axis=0, tiled=True)  1.84 us
  transfers between devices with their start and end apart: 7, of which 7 were waited for; matrix products, arithmetic and copies ran while one was open for 0% of the time, Pallas kernels for 0%

profile of v1, /device:TPU:0, one launch (start us, length us, event | category | flops | bytes accessed | tf_op | source)
XLA Modules:
  0.0 58.7 jit_solution(11480057375661233241)
XLA Ops:
  0.0 0.0 copy-start
  0.0 0.0 copy-start.1
  0.0 1.0 %convert_reduce_fusion = f32[32,4]{1,0:T(8,128)S(1)} fusion(bf16[32,4,256]{2,1,0:T(4,128)(2,1)} %param.6), kind=kLoop, calls=%fused_computation.6 | loop fusion | flops 65408 | bytes 66048 | tf_op jit(solution)/shard_map/reduce_sum | solution.py:10
  1.0 0.0 copy-done.1
  1.1 0.2 fusion.4
  1.2 0.0 copy-start.4
  1.3 0.7 %copy-done.4 = f32[256]{0:T(256)S(1)} copy-done((f32[256]{0:T(256)S(1)}, f32[256]{0:T(256)}, u32[]{:S(2)}) %copy-start.4) | copy-done | bytes 1048
  1.9 0.1 fusion.6
  2.1 0.0 copy-start.2
  2.1 0.0 copy-start.3
  2.1 0.7 %copy-done.2 = bf16[256,32]{0,1:T(8,128)(2,1)S(1)} copy-done((bf16[256,32]{0,1:T(8,128)(2,1)S(1)}, bf16[256,32]{0,1:T(8,128)(2,1)}, u32[]{:S(2)}) %copy-start.2) | copy-done | bytes 16408
  2.8 0.0 copy-done.3
  2.8 0.1 convolution_convert_fusion
  2.9 0.1 copy.12
  3.1 0.1 fusion.11
  3.2 3.0 %collective-permute-start = (bf16[32,4,32]{2,1,0:T(4,128)(2,1)S(1)}, bf16[32,4,32]{2,1,0:T(4,128)(2,1)S(1)}, u32[]{:S(2)}, u32[]{:S(2)}) collective-permute-start(bf16[32,4,32]{2,1,0:T(4,128)(2,1)S(1)} %get-tuple-element.15), channel_id=1, source_target_pairs={{0,2},{2,4},{4,6},{6,8},{8,10},{10,12},{12,14},{14,0},{1,3},{3,5},... | collective-permute-start | bytes 24584 | tf_op jit(solution)/shard_map/ppermute | solution.py:62
  6.2 4.9 %collective-permute-done = bf16[32,4,32]{2,1,0:T(4,128)(2,1)S(1)} collective-permute-done((bf16[32,4,32]{2,1,0:T(4,128)(2,1)S(1)}, bf16[32,4,32]{2,1,0:T(4,128)(2,1)S(1)}, u32[]{:S(2)}, u32[]{:S(2)}) %collective-permute-start) | collective-permute-done | bytes 8224 | tf_op jit(solution)/shard_map/ppermute | solution.py:62
  11.1 0.0 collective-permute-start.1
  11.1 6.6 %collective-permute-done.1 = bf16[32,4,32]{2,1,0:T(4,128)(2,1)S(1)} collective-permute-done((bf16[32,4,32]{2,1,0:T(4,128)(2,1)S(1)}, bf16[32,4,32]{2,1,0:T(4,128)(2,1)S(1)}, u32[]{:S(2)}, u32[]{:S(2)}) %collective-permute-start.1) | collective-permute-done | bytes 8224 | tf_op jit(solution)/shard_map/ppermute | solution.py:62
  17.7 0.0 collective-permute-start.2
  17.7 6.6 %collective-permute-done.2 = bf16[32,4,32]{2,1,0:T(4,128)(2,1)S(1)} collective-permute-done((bf16[32,4,32]{2,1,0:T(4,128)(2,1)S(1)}, bf16[32,4,32]{2,1,0:T(4,128)(2,1)S(1)}, u32[]{:S(2)}, u32[]{:S(2)}) %collective-permute-start.2) | collective-permute-done | bytes 8224 | tf_op jit(solution)/shard_map/ppermute | solution.py:62
  24.3 0.0 collective-permute-start.3
  24.4 6.6 %collective-permute-done.3 = bf16[32,4,32]{2,1,0:T(4,128)(2,1)S(1)} collective-permute-done((bf16[32,4,32]{2,1,0:T(4,128)(2,1)S(1)}, bf16[32,4,32]{2,1,0:T(4,128)(2,1)S(1)}, u32[]{:S(2)}, u32[]{:S(2)}) %collective-permute-start.3) | collective-permute-done | bytes 8224 | tf_op jit(solution)/shard_map/ppermute | solution.py:62
  31.0 0.0 collective-permute-start.4
  31.0 6.9 %collective-permute-done.4 = bf16[32,4,32]{2,1,0:T(4,128)(2,1)S(1)} collective-permute-done((bf16[32,4,32]{2,1,0:T(4,128)(2,1)S(1)}, bf16[32,4,32]{2,1,0:T(4,128)(2,1)S(1)}, u32[]{:S(2)}, u32[]{:S(2)}) %collective-permute-start.4) | collective-permute-done | bytes 8224 | tf_op jit(solution)/shard_map/ppermute | solution.py:62
  37.9 0.0 collective-permute-start.5
  37.9 6.6 %collective-permute-done.5 = bf16[32,4,32]{2,1,0:T(4,128)(2,1)S(1)} collective-permute-done((bf16[32,4,32]{2,1,0:T(4,128)(2,1)S(1)}, bf16[32,4,32]{2,1,0:T(4,128)(2,1)S(1)}, u32[]{:S(2)}, u32[]{:S(2)}) %collective-permute-start.5) | collective-permute-done | bytes 8224 | tf_op jit(solution)/shard_map/ppermute | solution.py:62
  44.5 0.0 collective-permute-start.6
  44.5 1.8 %all_gather.3 = bf16[64,4,32]{2,1,0:T(4,128)(2,1)S(1)} all-gather(bf16[32,4,32]{2,1,0:T(4,128)(2,1)S(1)} %get-tuple-element.16), channel_id=1, replica_groups=mesh['groups'=2,'res'=8,'seq'=2] {'seq'}, dimensions={0}, use_global_device_ids=true | all-gather | bytes 24576 | tf_op jit(solution)/shard_map/all_gather | solution.py:57
  46.4 0.1 copy.13
  46.5 4.7 %collective-permute-done.6 = bf16[32,4,32]{2,1,0:T(4,128)(2,1)S(1)} collective-permute-done((bf16[32,4,32]{2,1,0:T(4,128)(2,1)S(1)}, bf16[32,4,32]{2,1,0:T(4,128)(2,1)S(1)}, u32[]{:S(2)}, u32[]{:S(2)}) %collective-permute-start.6) | collective-permute-done | bytes 8224 | tf_op jit(solution)/shard_map/ppermute | solution.py:62
  51.1 0.5 concatenate.10
  51.7 0.1 constant_dynamic-slice_fusion
  51.8 0.3 reshape.50
  52.1 3.8 %all_to_all.15 = bf16[2,2,8192]{2,1,0:T(2,128)(2,1)S(1)} all-to-all(bf16[2,2,8192]{2,1,0:T(2,128)(2,1)S(1)} %reshape.50), channel_id=1, replica_groups=mesh['groups'=2,'res'=8,'seq'=2] {'seq'}, dimensions={0} | all-to-all | bytes 131072 | tf_op jit(solution)/shard_map/all_to_all | solution.py:69
  55.9 0.2 reshape.51
  56.1 0.2 reshape.47
  56.4 0.2 convolution_multiply_fusion
  56.5 0.3 reshape.48
  56.8 0.3 copy.15
  57.1 0.0 copy-start.5
  57.2 0.5 dot_general.15
  57.6 0.0 copy-done
  57.6 0.1 copy-done.5
  57.8 0.9 %fusion = bf16[4,16,128]{2,1,0:T(8,128)(2,1)} fusion(f32[4,16,1024]{2,1,0:T(8,128)S(1)} %dot_general.15, bf16[1024,128]{1,0:T(8,128)(2,1)S(1)} %copy-done, f32[128]{0:T(128)S(1)} %copy-done.5), kind=kOutput, calls=%fused_computation.3 | convolution fusion | flops 100679680 | bytes 541184 | tf_op jit(solution)/shard_map/while/body/eval_jaxpr/dot_general | solution.py:34
  (5 shorter events, 0.1 us)
Async XLA Ops:
  0.0 57.6 %copy-start = (bf16[1024,128]{1,0:T(8,128)(2,1)S(1)}, bf16[1024,128]{1,0:T(8,128)(2,1)}, u32[]{:S(2)}) copy-start(bf16[1024,128]{1,0:T(8,128)(2,1)} %param.10) | copy-start | bytes 786436
  0.0 1.0 %copy-start.1 = (bf16[32,4,256]{2,1,0:T(4,128)(2,1)S(1)}, bf16[32,4,256]{2,1,0:T(4,128)(2,1)}, u32[]{:S(2)}) copy-start(bf16[32,4,256]{2,1,0:T(4,128)(2,1)} %param.6) | copy-start | bytes 196612
  1.2 0.7 %copy-start.4 = (f32[256]{0:T(256)S(1)}, f32[256]{0:T(256)}, u32[]{:S(2)}) copy-start(f32[256]{0:T(256)} %param.7) | copy-start | bytes 3076
  2.1 0.7 %copy-start.2 = (bf16[256,32]{0,1:T(8,128)(2,1)S(1)}, bf16[256,32]{0,1:T(8,128)(2,1)}, u32[]{:S(2)}) copy-start(bf16[256,32]{0,1:T(8,128)(2,1)} %param.9) | copy-start | bytes 49156
  2.1 0.7 %copy-start.3 = (bf16[256,32]{0,1:T(8,128)(2,1)S(1)}, bf16[256,32]{0,1:T(8,128)(2,1)}, u32[]{:S(2)}) copy-start(bf16[256,32]{0,1:T(8,128)(2,1)} %param.8) | copy-start | bytes 49156
  3.2 8.0 %collective-permute-start = (bf16[32,4,32]{2,1,0:T(4,128)(2,1)S(1)}, bf16[32,4,32]{2,1,0:T(4,128)(2,1)S(1)}, u32[]{:S(2)}, u32[]{:S(2)}) collective-permute-start(bf16[32,4,32]{2,1,0:T(4,128)(2,1)S(1)} %get-tuple-element.15), channel_id=1, source_target_pairs={{0,2},{2,4},{4,6},{6,8},{8,10},{10,12},{12,14},{14,0},{1,3},{3,5},... | collective-permute-start | bytes 24584 | tf_op jit(solution)/shard_map/ppermute | solution.py:62
  11.1 6.6 %collective-permute-start.1 = (bf16[32,4,32]{2,1,0:T(4,128)(2,1)S(1)}, bf16[32,4,32]{2,1,0:T(4,128)(2,1)S(1)}, u32[]{:S(2)}, u32[]{:S(2)}) collective-permute-start(bf16[32,4,32]{2,1,0:T(4,128)(2,1)S(1)} %collective-permute-done), channel_id=1, source_target_pairs={{0,2},{2,4},{4,6},{6,8},{8,10},{10,12},{12,14},{14,0},{1,3},{3,5},... | collective-permute-start | bytes 24584 | tf_op jit(solution)/shard_map/ppermute | solution.py:62
  17.7 6.6 %collective-permute-start.2 = (bf16[32,4,32]{2,1,0:T(4,128)(2,1)S(1)}, bf16[32,4,32]{2,1,0:T(4,128)(2,1)S(1)}, u32[]{:S(2)}, u32[]{:S(2)}) collective-permute-start(bf16[32,4,32]{2,1,0:T(4,128)(2,1)S(1)} %collective-permute-done.1), channel_id=1, source_target_pairs={{0,2},{2,4},{4,6},{6,8},{8,10},{10,12},{12,14},{14,0},{1,3},{3,5},... | collective-permute-start | bytes 24584 | tf_op jit(solution)/shard_map/ppermute | solution.py:62
  24.3 6.6 %collective-permute-start.3 = (bf16[32,4,32]{2,1,0:T(4,128)(2,1)S(1)}, bf16[32,4,32]{2,1,0:T(4,128)(2,1)S(1)}, u32[]{:S(2)}, u32[]{:S(2)}) collective-permute-start(bf16[32,4,32]{2,1,0:T(4,128)(2,1)S(1)} %collective-permute-done.2), channel_id=1, source_target_pairs={{0,2},{2,4},{4,6},{6,8},{8,10},{10,12},{12,14},{14,0},{1,3},{3,5},... | collective-permute-start | bytes 24584 | tf_op jit(solution)/shard_map/ppermute | solution.py:62
  31.0 7.0 %collective-permute-start.4 = (bf16[32,4,32]{2,1,0:T(4,128)(2,1)S(1)}, bf16[32,4,32]{2,1,0:T(4,128)(2,1)S(1)}, u32[]{:S(2)}, u32[]{:S(2)}) collective-permute-start(bf16[32,4,32]{2,1,0:T(4,128)(2,1)S(1)} %collective-permute-done.3), channel_id=1, source_target_pairs={{0,2},{2,4},{4,6},{6,8},{8,10},{10,12},{12,14},{14,0},{1,3},{3,5},... | collective-permute-start | bytes 24584 | tf_op jit(solution)/shard_map/ppermute | solution.py:62
  37.9 6.6 %collective-permute-start.5 = (bf16[32,4,32]{2,1,0:T(4,128)(2,1)S(1)}, bf16[32,4,32]{2,1,0:T(4,128)(2,1)S(1)}, u32[]{:S(2)}, u32[]{:S(2)}) collective-permute-start(bf16[32,4,32]{2,1,0:T(4,128)(2,1)S(1)} %collective-permute-done.4), channel_id=1, source_target_pairs={{0,2},{2,4},{4,6},{6,8},{8,10},{10,12},{12,14},{14,0},{1,3},{3,5},... | collective-permute-start | bytes 24584 | tf_op jit(solution)/shard_map/ppermute | solution.py:62
  44.5 6.6 %collective-permute-start.6 = (bf16[32,4,32]{2,1,0:T(4,128)(2,1)S(1)}, bf16[32,4,32]{2,1,0:T(4,128)(2,1)S(1)}, u32[]{:S(2)}, u32[]{:S(2)}) collective-permute-start(bf16[32,4,32]{2,1,0:T(4,128)(2,1)S(1)} %collective-permute-done.5), channel_id=1, source_target_pairs={{0,2},{2,4},{4,6},{6,8},{8,10},{10,12},{12,14},{14,0},{1,3},{3,5},... | collective-permute-start | bytes 24584 | tf_op jit(solution)/shard_map/ppermute | solution.py:62
  57.1 0.7 %copy-start.5 = (f32[128]{0:T(128)S(1)}, f32[128]{0:T(128)}, u32[]{:S(2)}) copy-start(f32[128]{0:T(128)} %param.11) | copy-start | bytes 1540
